TPU v7x, 32 devices: a whole 2x2x4 slice. The times are simulated.
32 devices in a mesh: dp: 8 (over y, x, core), mp: 4 (over z).
Axes of the slice: x: 2, y: 2, z: 4, core: 2. Of those that a mesh axis runs over, the one named last changes fastest.
Arguments:
- hidden: bfloat16 [16384, 13824], P('dp', 'mp'), may hold values from -6 to 6
- out_grad: bfloat16 [16384, 5120], P('dp', 'mp'), may hold values from -6 to 6
- proj_in: bfloat16 [64, 13824], P(None, 'mp'), may hold values from -0.0546875 to 0.0546875
- proj_out: bfloat16 [64, 5120], P(None, 'mp'), may hold values from -0.078125 to 0.078125
- segment_ids: int32 [8, 2048], P('dp'), may hold values from 0 to 15, never falling along the last dimension, each value on 1 to 1024 neighbouring positions
Outputs:
- features: float32 [128, 4096], P('dp')
- gram: float32 [4096, 4096], P(('dp', 'mp'))
Inputs may be any that keep to these rules, and one draw needn't show every extreme that they name: `segment_ids`: within each row the numbers never fall; each of the 16 numbers names 1 to 1024 tokens of the row.
All inputs are finite; a program needn't handle non-finite values.
Results may differ from a plain program's by a relative error of at most 0.0003.
Values sent between devices are 32-bit elements; how exact they have to be, the bound alone decides.
No kernel may reach another device: no remote copies, remote signals or barrier semaphores. Data moves between devices by JAX's collectives and lax.ppermute only.
A program may use at most 64 MiB of HBM per device.

v0:
```python
import jax
import jax.numpy as jnp
from jax import lax
from jax.sharding import PartitionSpec as P

EX_DEV = 16


def outer_sums(onehot, projected, width):
    inputs = projected[:, :width]
    outputs = projected[:, width:]
    weighted = onehot[:, :, None] * outputs[None, :, :]
    grads = jnp.einsum("eti,tj->eij", weighted, inputs, precision=lax.Precision.HIGHEST)
    return grads.reshape(onehot.shape[0], width * width)


def body(hidden, out_grad, proj_in, proj_out, segment_ids):
    width = proj_in.shape[0]
    examples = EX_DEV
    inputs = lax.dot_general(
        hidden, proj_in, (((1,), (1,)), ((), ())), preferred_element_type=jnp.float32
    )
    outputs = lax.dot_general(
        out_grad, proj_out, (((1,), (1,)), ((), ())), preferred_element_type=jnp.float32
    )
    projected = jnp.concatenate([inputs, outputs], axis=1)
    example_ids = segment_ids[0]
    onehot = (example_ids[None, :] == jnp.arange(examples, dtype=jnp.int32)[:, None]).astype(
        jnp.float32
    )
    counts = jnp.sum(onehot, axis=1)
    summed = lax.psum(projected, "mp")
    grads = outer_sums(onehot, summed, width)
    features = grads / jnp.sqrt(counts)[:, None]
    proj_size = width * width
    data_count = lax.axis_size("dp")
    model_count = lax.axis_size("mp")
    row_count = proj_size // (data_count * model_count)
    total_examples = examples * data_count
    col_first = (lax.axis_index("dp") * model_count + lax.axis_index("mp")) * row_count
    shard_piece = lax.all_gather(features, "dp", axis=0, tiled=True)
    left = lax.dynamic_slice_in_dim(shard_piece, col_first, row_count, 1)
    gram_rows = lax.dot_general(
        left,
        shard_piece,
        (((0,), (0,)), ((), ())),
        precision=lax.Precision.HIGHEST,
        preferred_element_type=jnp.float32,
    )
    return (features, gram_rows / total_examples)


def solution(mesh):
    placed = (P("dp", "mp"), P("dp", "mp"), P(None, "mp"), P(None, "mp"), P("dp", None))
    return jax.shard_map(
        body,
        mesh=mesh,
        in_specs=placed,
        out_specs=(P("dp", None), P(("dp", "mp"), None)),
        check_vma=False,
    )
```

profile of v0, /device:TPU:0, one launch (start us, length us, event | category | flops | bytes accessed | tf_op | source)
XLA Modules:
  0.0 124.1 jit_solution(2751535235130744079)
XLA Ops:
  7.2 0.0 copy-start
  7.2 0.0 copy-start.2
  7.2 0.0 all-reduce.2.cloned.1.call-start
  7.2 0.9 copy-done
  8.2 0.0 copy-start.1
  8.2 9.5 %fusion.8 = f32[2048,64]{0,1:T(8,128)S(1)} fusion(bf16[2048,3456]{1,0:T(8,128)(2,1)} %param.5, bf16[64,3456]{1,0:T(8,128)(2,1)S(1)} %copy-done), kind=kOutput, calls=%fused_computation.13 | convolution fusion | flops 905969664 | bytes 15122432 | tf_op jit(solution)/shard_map/dot_general | solution.py:20
  17.7 0.0 copy-done.2
  17.7 0.0 copy-done.1
  17.7 0.0 copy-start.3
  17.8 1.7 %fusion.9 = f32[2048,64]{0,1:T(8,128)S(1)} fusion(bf16[2048,1280]{1,0:T(8,128)(2,1)S(1)} %copy-done.1, bf16[64,1280]{1,0:T(8,128)(2,1)S(1)} %copy-done.2), kind=kOutput, calls=%fused_computation.14 | convolution fusion | flops 335544320 | bytes 5931008 | tf_op jit(solution)/shard_map/dot_general | solution.py:23
  19.4 1.1 pad_maximum_fusion
  20.5 0.0 all-reduce.2.cloned.1.call-update
  20.5 0.2 all-gather.2.cloned.1.call-start
  20.8 0.0 copy-done.3
  20.8 0.1 fusion.6
  20.9 54.4 %all-reduce.2.cloned.1.call-done = f32[2048,128]{0,1:T(8,128)} async-done(((f32[2048,128]{0,1:T(8,128)}), f32[2048,128]{0,1:T(8,128)}) %all-reduce.2.cloned.1.call-update) | async-done | bytes 1048592 | tf_op jit(solution)/shard_map/psum | solution.py:32
  75.4 1.1 slice.8
  76.4 7.7 %fusion = f32[16,64,64]{2,1,0:T(8,128)S(1)} fusion(f32[2048,64]{0,1:T(8,128)S(1)} %slice.8, f32[16,2048]{1,0:T(8,128)S(1)} %fusion.4, f32[2048,128]{0,1:T(8,128)} %all-reduce.2.cloned.1.call-done), kind=kOutput, calls=%fused_computation | convolution fusion | flops 1612709888 | bytes 1441792 | tf_op jit(solution)/shard_map/eti,tj->eij/dot_general | solution.py:13
  84.1 0.2 reshape.32
  84.3 0.8 broadcast_divide_fusion
  85.1 0.0 all-gather.2.cloned.1.call-update
  85.1 27.2 %all-gather.2.cloned.1.call-done = f32[128,4096]{1,0:T(8,128)} async-done(((f32[16,4096]{1,0:T(8,128)}), f32[128,4096]{1,0:T(8,128)}) %all-gather.2.cloned.1.call-update) | async-done | bytes 2097168 | tf_op jit(solution)/shard_map/all_gather | solution.py:41
  112.3 4.9 %convolution_multiply_fusion = f32[128,4096]{1,0:T(8,128)} fusion(f32[128,4096]{1,0:T(8,128)} %all-gather.2.cloned.1.call-done, s32[]{:T(128)S(6)} %select_n.3), kind=kOutput, calls=%fused_computation.2 | convolution fusion | flops 805830656 | bytes 4259844 | tf_op jit(solution)/shard_map/dot_general | solution.py:43
  (2 shorter events, 0.0 us)
Async XLA Ops:
  7.2 1.0 copy-start
  7.2 10.5 %copy-start.2 = (bf16[64,1280]{1,0:T(8,128)(2,1)S(1)}, bf16[64,1280]{1,0:T(8,128)(2,1)}, u32[]{:S(2)}) copy-start(bf16[64,1280]{1,0:T(8,128)(2,1)} %param.8) | copy-start | bytes 491524
  7.2 68.2 %all-reduce.2.cloned.1.call-start = ((), (), s32[]{:S(2)}) async-start(), calls=%async_computation | async-start | bytes 2097152 | tf_op jit(solution)/shard_map/psum | solution.py:32
  8.2 9.5 %copy-start.1 = (bf16[2048,1280]{1,0:T(8,128)(2,1)S(1)}, bf16[2048,1280]{1,0:T(8,128)(2,1)}, u32[]{:S(2)}) copy-start(bf16[2048,1280]{1,0:T(8,128)(2,1)} %param.6) | copy-start | bytes 15728644
  17.7 3.0 %copy-start.3 = (s32[1,2048]{1,0:T(1,128)S(1)}, s32[1,2048]{1,0:T(1,128)}, u32[]{:S(2)}) copy-start(s32[1,2048]{1,0:T(1,128)} %param.9) | copy-start | bytes 24580
  20.5 91.8 %all-gather.2.cloned.1.call-start = ((), (), s32[]{:S(2)}) async-start(), calls=%async_computation.1 | async-start | bytes 2359296 | tf_op jit(solution)/shard_map/all_gather | solution.py:41
Sparse Core Ops, SparseCore 0:
  20.6 54.6 all-reduce.1
  85.2 27.0 all-gather.1
where the time goes:
time: 124 us
  waiting for transfers between devices  81.7 us (66%)
  matrix products  23.8 us (19%)
  between operations  14.1 us (11%)
  local copies, waits for them, and re-layouts  2.24 us (2%)
  other arithmetic  2 us (2%)
    psum x1, waiting for transfers between devices, body(): summed = lax.psum(projected, 'mp')  54.4 us
    all_gather x1, waiting for transfers between devices, body(): shard_piece = lax.all_gather(features, 'dp', axis=0, tiled=True)  27.2 us
    dot_general x1, matrix products, body(): lax.dot_general(hidden, proj_in, (((1,), (1,)), ((), ())), preferred_elem...  9.53 us
    dot_general x1, matrix products, outer_sums(): jnp.einsum('eti,tj->eij', weighted, inputs, precision=lax.Precision.HIGHEST)  7.67 us
    dot_general x1, matrix products, body(): lax.dot_general(left, shard_piece, (((0,), (0,)), ((), ())), precision=la...  4.89 us
  transfers between devices with their start and end apart: 2, of which 2 were waited for; matrix products, arithmetic and copies ran while one was open for 0% of the time, Pallas kernels for 0%

commit v1 on v0

--- a/solution.py
+++ b/solution.py
@@ -29,7 +29,7 @@
         jnp.float32
     )
     counts = jnp.sum(onehot, axis=1)
-    summed = lax.psum(projected, "mp")
+    summed = jax.lax.all_gather(projected, axis_name="mp").sum(axis=0)
     grads = outer_sums(onehot, summed, width)
     features = grads / jnp.sqrt(counts)[:, None]
     proj_size = width * width

time: 124 us -> 163 us (1.31)
  waiting for transfers between devices: 81.7 us -> 110 us
  other arithmetic: 2 us -> 6.86 us
  local copies, waits for them, and re-layouts: 2.24 us -> 6.28 us
    all_gather x0 -> x1, waiting for transfers between devices: none -> 83.4 us  [body(): summed = jax.lax.all_gather(projected, axis_name='mp').sum(axis=0)]
    psum x1 -> x0, waiting for transfers between devices: 54.4 us -> none  [body(): summed = lax.psum(projected, 'mp')]
    all_gather x0 -> x1, local copies, waits for them, and re-layouts: none -> 6.03 us  [body(): summed = jax.lax.all_gather(projected, axis_name='mp').sum(axis=0)]
    reduce_sum x0 -> x1, other arithmetic: none -> 4.84 us  [body(): summed = jax.lax.all_gather(projected, axis_name='mp').sum(axis=0)]
    dot_general x1, matrix products: 1.68 us -> 4.21 us  [body(): lax.dot_general(out_grad, proj_out, (((1,), (1,)), ((), ())), preferred_e...]
where the time goes in v1:
time: 163 us; the launch traced here: 162 us
  waiting for transfers between devices  110 us (67%)
  matrix products  25.1 us (15%)
  between operations  14.1 us (9%)
  other arithmetic  6.86 us (4%)
  local copies, waits for them, and re-layouts  6.28 us (4%)
    all_gather x1, waiting for transfers between devices, body(): summed = jax.lax.all_gather(projected, axis_name='mp').sum(axis=0)  83.4 us
    all_gather x1, waiting for transfers between devices, body(): shard_piece = lax.all_gather(features, 'dp', axis=0, tiled=True)  26.4 us
    dot_general x1, matrix products, body(): lax.dot_general(hidden, proj_in, (((1,), (1,)), ((), ())), preferred_elem...  9.39 us
    dot_general x1, matrix products, outer_sums(): jnp.einsum('eti,tj->eij', weighted, inputs, precision=lax.Precision.HIGHEST)  6.63 us
    all_gather x1, local copies, waits for them, and re-layouts, body(): summed = jax.lax.all_gather(projected, axis_name='mp').sum(axis=0)  6.03 us
    dot_general x1, matrix products, body(): lax.dot_general(left, shard_piece, (((0,), (0,)), ((), ())), precision=la...  4.89 us
    reduce_sum x1, other arithmetic, body(): summed = jax.lax.all_gather(projected, axis_name='mp').sum(axis=0)  4.84 us
    dot_general x1, matrix products, body(): lax.dot_general(out_grad, proj_out, (((1,), (1,)), ((), ())), preferred_e...  4.21 us
  transfers between devices with their start and end apart: 2, of which 2 were waited for; matrix products, arithmetic and copies ran while one was open for 0% of the time, Pallas kernels for 0%

profile of v1, /device:TPU:0, one launch (start us, length us, event | category | flops | bytes accessed | tf_op | source)
XLA Modules:
  0.0 162.3 jit_solution(8876331291347958998)
XLA Ops:
  7.2 0.0 copy-start
  7.2 0.0 all-gather.6.cloned.1.call-start
  7.2 4.2 %fusion.9 = f32[2048,64]{0,1:T(8,128)S(1)} fusion(bf16[2048,1280]{1,0:T(8,128)(2,1)} %param.6, bf16[64,1280]{1,0:T(8,128)(2,1)} %param.8), kind=kOutput, calls=%fused_computation.14 | convolution fusion | flops 335544320 | bytes 5931008 | tf_op jit(solution)/shard_map/dot_general | solution.py:23
  11.4 0.0 copy-done
  11.5 0.0 copy-start.1
  11.5 9.4 %fusion.8 = f32[2048,64]{0,1:T(8,128)S(1)} fusion(bf16[2048,3456]{1,0:T(8,128)(2,1)} %param.5, bf16[64,3456]{1,0:T(8,128)(2,1)S(1)} %copy-done), kind=kOutput, calls=%fused_computation.13 | convolution fusion | flops 905969664 | bytes 15122432 | tf_op jit(solution)/shard_map/dot_general | solution.py:20
  20.9 1.1 pad_maximum_fusion
  21.9 0.0 all-gather.6.cloned.1.call-update
  22.0 0.0 all-gather.4.cloned.1.call-start
  22.0 0.0 copy-done.1
  22.0 0.1 fusion.6
  22.2 83.4 %all-gather.6.cloned.1.call-done = f32[8192,128]{0,1:T(8,128)} async-done(((f32[2048,128]{0,1:T(8,128)}), f32[8192,128]{0,1:T(8,128)}) %all-gather.6.cloned.1.call-update) | async-done | bytes 4194320 | tf_op jit(solution)/shard_map/all_gather | solution.py:32
  105.6 6.0 %reshape.33 = f32[4,2048,128]{1,0,2:T(4,128)} reshape(f32[8192,128]{0,1:T(8,128)} %all-gather.6.cloned.1.call-done) | data formatting | bytes 8388608 | tf_op jit(solution)/shard_map/all_gather | solution.py:32
  111.6 4.8 %reduce_sum.18 = f32[2048,128]{0,1:T(8,128)S(1)} reduce(f32[4,2048,128]{1,0,2:T(4,128)} %reshape.33, f32[]{:T(128)} %constant.4.clone.1), dimensions={0}, to_apply=%region_0.0 | reduce | flops 786432 | bytes 5242884 | tf_op jit(solution)/shard_map/reduce_sum | solution.py:32
  116.5 6.6 %fusion = f32[16,64,64]{2,1,0:T(8,128)S(1)} fusion(f32[2048,64]{0,1:T(8,128)S(1)} %slice.8, f32[16,2048]{1,0:T(8,128)S(1)} %fusion.4, f32[2048,128]{0,1:T(8,128)S(1)} %reduce_sum.18), kind=kOutput, calls=%fused_computation | convolution fusion | flops 1612709888 | bytes 1441792 | tf_op jit(solution)/shard_map/eti,tj->eij/dot_general | solution.py:13
  123.1 0.2 reshape.32
  123.3 0.8 broadcast_divide_fusion
  124.1 0.0 all-gather.4.cloned.1.call-update
  124.1 26.4 %all-gather.4.cloned.1.call-done = f32[128,4096]{1,0:T(8,128)} async-done(((f32[16,4096]{1,0:T(8,128)}), f32[128,4096]{1,0:T(8,128)}) %all-gather.4.cloned.1.call-update) | async-done | bytes 2097168 | tf_op jit(solution)/shard_map/all_gather | solution.py:41
  150.6 4.9 %convolution_multiply_fusion = f32[128,4096]{1,0:T(8,128)} fusion(f32[128,4096]{1,0:T(8,128)} %all-gather.4.cloned.1.call-done, s32[]{:T(128)S(6)} %select_n.3), kind=kOutput, calls=%fused_computation.2 | convolution fusion | flops 805830656 | bytes 4259844 | tf_op jit(solution)/shard_map/dot_general | solution.py:43
  (3 shorter events, 0.1 us)
Async XLA Ops:
  7.2 4.3 %copy-start = (bf16[64,3456]{1,0:T(8,128)(2,1)S(1)}, bf16[64,3456]{1,0:T(8,128)(2,1)}, u32[]{:S(2)}) copy-start(bf16[64,3456]{1,0:T(8,128)(2,1)} %param.7) | copy-start | bytes 1327108
  7.2 98.4 %all-gather.6.cloned.1.call-start = ((), (), s32[]{:S(2)}) async-start(), calls=%async_computation.1 | async-start | bytes 5242880 | tf_op jit(solution)/shard_map/all_gather | solution.py:32
  11.5 10.6 %copy-start.1 = (s32[1,2048]{1,0:T(1,128)S(1)}, s32[1,2048]{1,0:T(1,128)}, u32[]{:S(2)}) copy-start(s32[1,2048]{1,0:T(1,128)} %param.9) | copy-start | bytes 24580
  22.0 128.6 %all-gather.4.cloned.1.call-start = ((), (), s32[]{:S(2)}) async-start(), calls=%async_computation | async-start | bytes 2359296 | tf_op jit(solution)/shard_map/all_gather | solution.py:41
Sparse Core Ops, SparseCore 0:
  22.1 83.4 all-gather.5
  124.3 26.2 all-gather.3
